TPU v7x, 32 devices: a whole 2x2x4 slice. The times are simulated.
32 devices in a mesh: groups: 2 (over y), tensor: 4 (over z), frames: 4 (over x, core).
Axes of the slice: x: 2, y: 2, z: 4, core: 2. Of those that a mesh axis runs over, the one named last changes fastest.
Arguments:
- patches: bfloat16 [256, 16, 3072], P('tensor', ('groups', 'frames')), parts along dimension 1, may hold values from -12 to 12
- ln_gain: float32 [3072], replicated, may hold values from 0.5 to 1.5
- in_weight: bfloat16 [3072, 4, 768], P('frames', 'tensor'), may hold values from -0.109375 to 0.109375
- q_gain: float32 [4, 128], P('tensor'), may hold values from 0.1 to 1.9
- k_gain: float32 [4, 128], P('tensor'), may hold values from 0.1 to 1.9
- out_weight: bfloat16 [4, 512, 3072], P('tensor', None, 'frames'), may hold values from -0.25 to 0.25
Outputs:
- encoded: bfloat16 [256, 16, 3072], P('tensor', ('groups', 'frames')), parts along dimension 1
There are 2 independent parts, one for each index of `groups`. A program takes and returns all parts, laid end to end along the dimension named above; an argument that names none is the same for every part. Nothing has to cross between parts.
All inputs are finite; a program needn't handle non-finite values.
Results may differ from a plain program's by a relative error of at most 0.022.
Values may be sent and summed in bfloat16 or wider, within the bound.
No kernel may reach another device: no remote copies, remote signals or barrier semaphores. Data moves between devices by JAX's collectives and lax.ppermute only.
A program may use at most 64 MiB of HBM per device.

v0:
```python
import math
import jax
import jax.numpy as jnp
from jax import lax
from jax.sharding import PartitionSpec as P


def layer_norm(values, gain_vec):
    mean_val = jnp.mean(values, axis=-1, keepdims=True)
    centered = values - mean_val
    variance = jnp.mean(centered * centered, axis=-1, keepdims=True)
    return centered * lax.rsqrt(variance + 1e-06) * gain_vec


def local(patches, ln_gain, in_weight, q_gain, k_gain, out_weight):
    head_dim = q_gain.shape[1]
    normed = layer_norm(patches.astype(jnp.float32), ln_gain).astype(jnp.bfloat16)
    in_local = in_weight[:, 0, :]
    out_local = out_weight[0]
    every_patch = lax.all_gather(normed, "tensor", axis=0, tiled=True)
    joined_cols = jnp.einsum(
        "qye,ea->qya",
        every_patch,
        lax.all_gather(in_local, "frames", axis=0, tiled=True),
        preferred_element_type=jnp.float32,
    )
    query_slice = layer_norm(joined_cols[..., :head_dim], q_gain[0])
    key_slice = layer_norm(joined_cols[..., head_dim : 2 * head_dim], k_gain[0])
    value_slice = joined_cols[..., 2 * head_dim : 3 * head_dim]
    hidden = jax.nn.gelu(joined_cols[..., 3 * head_dim :], approximate=False)
    prepared = jnp.concatenate([query_slice, key_slice, value_slice, hidden], axis=-1).astype(
        jnp.bfloat16
    )
    query_slice = prepared[..., :head_dim]
    key_slice = prepared[..., head_dim : 2 * head_dim]
    value_slice = prepared[..., 2 * head_dim : 3 * head_dim]
    attention_logits = jnp.einsum(
        "ldg,bdg->dlb", query_slice, key_slice, preferred_element_type=jnp.float32
    ) * (1.0 / math.sqrt(head_dim))
    exponent_scores = jnp.exp(attention_logits)
    softmax_total = jnp.sum(exponent_scores, axis=-1)
    attention_output = jnp.einsum(
        "jdl,ljg->djg",
        exponent_scores.astype(jnp.bfloat16),
        value_slice,
        preferred_element_type=jnp.float32,
    )
    attention_output = attention_output / jnp.transpose(softmax_total)[:, :, None]
    blended_rows = jnp.concatenate(
        [attention_output.astype(jnp.bfloat16), prepared[..., 3 * head_dim :]], axis=-1
    )
    combined_output = lax.all_gather(out_local, "frames", axis=1, tiled=True)
    summed = lax.psum_scatter(
        jnp.einsum(
            "vto,ox->vtx", blended_rows, combined_output, preferred_element_type=jnp.float32
        ).astype(jnp.bfloat16),
        "tensor",
        scatter_dimension=0,
        tiled=True,
    ).astype(jnp.float32)
    return (patches.astype(jnp.float32) + summed).astype(jnp.bfloat16)


def solution(mesh):
    return jax.shard_map(
        local,
        mesh=mesh,
        in_specs=(
            P("tensor", ("groups", "frames"), None),
            P(),
            P("frames", "tensor", None),
            P("tensor", None),
            P("tensor", None),
            P("tensor", None, "frames"),
        ),
        out_specs=P("tensor", ("groups", "frames"), None),
        check_vma=False,
    )
```

profile of v0, /device:TPU:0, one launch (start us, length us, event | category | flops | bytes accessed | tf_op | source)
XLA Modules:
  0.0 220.3 jit_solution(9089769881547310153)
XLA Ops:
  6.5 1.4 convert_reduce_fusion
  7.9 1.5 fusion.5
  9.5 1.2 fusion.7
  10.7 0.0 all-gather.6.cloned.1.call-update
  10.7 0.0 all-gather.8.cloned.1.call-start
  10.8 0.7 all-gather.8.cloned.1.call-update
  11.5 0.0 all-gather.10.cloned.1.call-start
  11.5 0.7 all-gather.10.cloned.1.call-update
  12.2 0.0 copy-start.2
  12.2 0.0 reduce-scatter.2.cloned.1.call-start
  12.3 64.8 %all-gather.6.cloned.1.call-done = bf16[256,2,3072]{2,0,1:T(8,128)(2,1)} async-done(((bf16[64,2,3072]{2,0,1:T(8,128)(2,1)}), bf16[256,2,3072]{2,0,1:T(8,128)(2,1)}) %all-gather.6.cloned.1.call-update) | async-done | bytes 3145744 | tf_op jit(solution)/shard_map/all_gather | solution.py:20
  77.0 37.7 %all-gather.8.cloned.1.call-done = bf16[3072,1,768]{2,0,1:T(8,128)(2,1)} async-done(((bf16[768,1,768]{2,0,1:T(8,128)(2,1)}), bf16[3072,1,768]{2,0,1:T(8,128)(2,1)}) %all-gather.8.cloned.1.call-update) | async-done | bytes 4718608 | tf_op jit(solution)/shard_map/all_gather | solution.py:24
  114.7 5.9 %fusion = f32[256,2,768]{2,0,1:T(8,128)S(1)} fusion(bf16[256,2,3072]{2,0,1:T(8,128)(2,1)} %all-gather.6.cloned.1.call-done, bf16[3072,1,768]{2,0,1:T(8,128)(2,1)} %all-gather.8.cloned.1.call-done), kind=kOutput, calls=%fused_computation | convolution fusion | flops 2415919104 | bytes 9437184 | tf_op jit(solution)/shard_map/qye,ea->qya/dot_general | solution.py:21
  120.6 0.2 slice_reduce_fusion.1
  120.8 0.4 multiply_reduce_fusion.1
  121.3 0.5 fusion.33
  121.8 0.3 fusion.11
  122.0 1.7 fusion.14
  123.8 21.1 %all-gather.10.cloned.1.call-done = bf16[1,512,3072]{2,1,0:T(8,128)(2,1)} async-done(((bf16[1,512,768]{2,1,0:T(8,128)(2,1)}), bf16[1,512,3072]{2,1,0:T(8,128)(2,1)}) %all-gather.10.cloned.1.call-update) | async-done | bytes 3145744 | tf_op jit(solution)/shard_map/all_gather | solution.py:52
  144.8 5.4 %convolution_convert_fusion = bf16[256,2,3072]{2,0,1:T(8,128)(2,1)} fusion(bf16[1,512,3072]{2,1,0:T(8,128)(2,1)} %all-gather.10.cloned.1.call-done, bf16[256,2,384]{2,0,1:T(8,128)(2,1)S(1)} %fusion.14, bf16[256,2,128]{2,0,1:T(8,128)(2,1)S(1)} %fusion.11), kind=kOutput, calls=%fused_computation.2 | convolution fusion | flops 1613234176 | bytes 6815744 | tf_op jit(solution)/shard_map/vto,ox->vtx/dot_general | solution.py:54
  150.2 0.0 reduce-scatter.2.cloned.1.call-update
  150.2 60.6 %reduce-scatter.2.cloned.1.call-done = bf16[64,2,3072]{2,0,1:T(8,128)(2,1)} async-done(((bf16[256,2,3072]{2,0,1:T(8,128)(2,1)}), bf16[64,2,3072]{2,0,1:T(8,128)(2,1)}) %reduce-scatter.2.cloned.1.call-update) | async-done | bytes 786448 | tf_op jit(solution)/shard_map/reduce_scatter | solution.py:53
  210.8 1.3 fusion.8
  212.1 1.7 copy.8
  (13 shorter events, 0.1 us)
Async XLA Ops:
  6.5 2.9 %copy-start = (bf16[64,2,3072]{2,1,0:T(2,128)(2,1)S(1)}, bf16[64,2,3072]{2,1,0:T(2,128)(2,1)}, u32[]{:S(2)}) copy-start(bf16[64,2,3072]{2,1,0:T(2,128)(2,1)} %param.6) | copy-start | bytes 2359300
  6.5 2.9 %copy-start.1 = (f32[3072]{0:T(1024)S(1)}, f32[3072]{0:T(1024)}, u32[]{:S(2)}) copy-start(f32[3072]{0:T(1024)} %param.7) | copy-start | bytes 36868
  6.5 70.5 %all-gather.6.cloned.1.call-start = ((), (), s32[]{:S(2)}) async-start(), calls=%async_computation.1 | async-start | bytes 3932160 | tf_op jit(solution)/shard_map/all_gather | solution.py:20
  10.7 104.0 %all-gather.8.cloned.1.call-start = ((), (), s32[]{:S(2)}) async-start(), calls=%async_computation.3 | async-start | bytes 5898240 | tf_op jit(solution)/shard_map/all_gather | solution.py:24
  11.5 133.3 %all-gather.10.cloned.1.call-start = ((), (), s32[]{:S(2)}) async-start(), calls=%async_computation.4 | async-start | bytes 3932160 | tf_op jit(solution)/shard_map/all_gather | solution.py:52
  12.2 109.0 %copy-start.2 = (f32[1,128]{1,0:T(1,128)S(1)}, f32[1,128]{1,0:T(1,128)}, u32[]{:S(2)}) copy-start(f32[1,128]{1,0:T(1,128)} %param.10) | copy-start | bytes 1540
  12.2 109.0 %copy-start.3 = (f32[1,128]{1,0:T(1,128)S(1)}, f32[1,128]{1,0:T(1,128)}, u32[]{:S(2)}) copy-start(f32[1,128]{1,0:T(1,128)} %param.9) | copy-start | bytes 1540
  12.2 198.5 %reduce-scatter.2.cloned.1.call-start = ((), (), s32[]{:S(2)}) async-start(), calls=%async_computation.2 | async-start | bytes 3932160 | tf_op jit(solution)/shard_map/reduce_scatter | solution.py:53
Sparse Core Ops, SparseCore 0:
  10.8 66.1 all-gather.5
  78.6 36.0 all-gather.7
  116.3 28.5 all-gather.9
  150.3 60.3 reduce-scatter.1
where the time goes:
time: 221 us; the launch traced here: 220 us
  waiting for transfers between devices  185 us (84%)
  between operations  13.2 us (6%)
  matrix products  12 us (5%)
  other arithmetic  7.81 us (4%)
    all_gather x1, waiting for transfers between devices, local(): every_patch = lax.all_gather(normed, 'tensor', axis=0, tiled=True)  64.8 us
    reduce_scatter x1, waiting for transfers between devices, local(): lax.psum_scatter(jnp.einsum('vto,ox->vtx', blended_rows, combined_output,...  60.6 us
    all_gather x1, waiting for transfers between devices, local(): lax.all_gather(in_local, 'frames', axis=0, tiled=True)  37.7 us
    all_gather x1, waiting for transfers between devices, local(): combined_output = lax.all_gather(out_local, 'frames', axis=1, tiled=True)  21.1 us
    dot_general x1, matrix products, local(): jnp.einsum('qye,ea->qya', every_patch, lax.all_gather(in_local, 'frames',...  5.89 us
    dot_general x1, matrix products, local(): jnp.einsum('vto,ox->vtx', blended_rows, combined_output, preferred_elemen...  5.36 us
  transfers between devices with their start and end apart: 4, of which 4 were waited for; matrix products, arithmetic and copies ran while one was open for 4% of the time, Pallas kernels for 0%

commit v1 on v0

--- a/solution.py
+++ b/solution.py
@@ -3,6 +3,7 @@
 import jax.numpy as jnp
 from jax import lax
 from jax.sharding import PartitionSpec as P
+from jax.lax import axis_index, axis_size, ppermute
 
 
 def layer_norm(values, gain_vec):
@@ -49,10 +50,34 @@
     blended_rows = jnp.concatenate(
         [attention_output.astype(jnp.bfloat16), prepared[..., 3 * head_dim :]], axis=-1
     )
-    combined_output = lax.all_gather(out_local, "frames", axis=1, tiled=True)
+
+    def group_spots(point, my_tile):
+        along_axis = "frames"
+        all_rows, mat_out, reached = (axis_size(along_axis), axis_index(along_axis), point.shape[1])
+        buffer = []
+        for dev_i in tuple(range(all_rows)):
+            buffer.append((dev_i, (dev_i + 1) % all_rows))
+        inter, d_next = (point, None)
+        for t in [*range(all_rows)]:
+            spare = (mat_out - t) % all_rows
+            state_next = ppermute(inter, along_axis, buffer) if t < all_rows - 1 else None
+            local_next = my_tile(inter, spare * reached)
+            state_now = local_next.shape[2]
+            if d_next is None:
+                d_next = jnp.zeros(
+                    (*local_next.shape[:2], all_rows * state_now, *local_next.shape[3:]),
+                    local_next.dtype,
+                )
+            d_next = lax.dynamic_update_slice_in_dim(d_next, local_next, spare * state_now, axis=2)
+            inter = state_next
+        return d_next
+
     summed = lax.psum_scatter(
-        jnp.einsum(
-            "vto,ox->vtx", blended_rows, combined_output, preferred_element_type=jnp.float32
+        group_spots(
+            out_local,
+            lambda part, offset: jnp.einsum(
+                "vto,ox->vtx", blended_rows, part, preferred_element_type=jnp.float32
+            ),
         ).astype(jnp.bfloat16),
         "tensor",
         scatter_dimension=0,

time: 221 us -> 203 us (0.919)
  waiting for transfers between devices: 185 us -> 164 us
  local copies, waits for them, and re-layouts: 1.71 us -> 5.04 us
    ppermute x0 -> x3, waiting for transfers between devices: none -> 23.1 us  [group_spots(): ppermute(inter, along_axis, buffer)]
    all_gather x1, waiting for transfers between devices: 64.8 us -> 41.9 us  [local(): every_patch = lax.all_gather(normed, 'tensor', axis=0, tiled=True)]
    all_gather x1 -> x0, waiting for transfers between devices: 21.1 us -> none  [local(): combined_output = lax.all_gather(out_local, 'frames', axis=1, tiled=True)]
    unnamed x8 -> x18, local copies, waits for them, and re-layouts: 0.02 us -> 2.99 us
    dot_general x1 -> x4, matrix products: 5.36 us -> 4.57 us  [local(): jnp.einsum('vto,ox->vtx', blended_rows, part, preferred_element_type=jnp....]
  transfers between devices with their start and end apart: 4 -> 6, of which waited for: 4 -> 5; matrix products, arithmetic and copies ran while one was open for 4% -> 6% of each run, Pallas kernels for 0% -> 0%
where the time goes in v1:
time: 203 us; the launch traced here: 202 us
  waiting for transfers between devices  164 us (81%)
  between operations  13.3 us (7%)
  matrix products  11.2 us (6%)
  other arithmetic  8.04 us (4%)
  local copies, waits for them, and re-layouts  5.04 us (2%)
    reduce_scatter x1, waiting for transfers between devices, local(): lax.psum_scatter(group_spots(out_local, lambda part, offset: jnp.einsum('...  60.6 us
    all_gather x1, waiting for transfers between devices, local(): every_patch = lax.all_gather(normed, 'tensor', axis=0, tiled=True)  41.9 us
    all_gather x1, waiting for transfers between devices, local(): lax.all_gather(in_local, 'frames', axis=0, tiled=True)  37.7 us
    ppermute x3, waiting for transfers between devices, group_spots(): ppermute(inter, along_axis, buffer)  23.1 us
    dot_general x1, matrix products, local(): jnp.einsum('qye,ea->qya', every_patch, lax.all_gather(in_local, 'frames',...  5.89 us
    dot_general x4, matrix products, local(): jnp.einsum('vto,ox->vtx', blended_rows, part, preferred_element_type=jnp....  4.57 us
  transfers between devices with their start and end apart: 6, of which 5 were waited for; matrix products, arithmetic and copies ran while one was open for 6% of the time, Pallas kernels for 0%

profile of v1, /device:TPU:0, one launch (start us, length us, event | category | flops | bytes accessed | tf_op | source)
XLA Modules:
  0.0 202.1 jit_solution(17286383190789408841)
XLA Ops:
  6.5 1.4 convert_reduce_fusion
  7.9 1.5 fusion.4
  9.5 1.2 fusion.6
  10.8 0.7 all-gather.6.cloned.1.call-update
  11.5 0.5 collective-permute-start
  12.1 11.6 %collective-permute-done = bf16[512,768]{1,0:T(8,128)(2,1)S(1)} collective-permute-done((bf16[512,768]{1,0:T(8,128)(2,1)S(1)}, bf16[512,768]{1,0:T(8,128)(2,1)S(1)}, u32[]{:S(2)}, u32[]{:S(2)}) %collective-permute-start) | collective-permute-done | bytes 786464 | tf_op jit(solution)/shard_map/ppermute | solution.py:63
  23.7 11.5 %collective-permute-done.1 = bf16[512,768]{1,0:T(8,128)(2,1)} collective-permute-done((bf16[512,768]{1,0:T(8,128)(2,1)S(1)}, bf16[512,768]{1,0:T(8,128)(2,1)}, u32[]{:S(2)}, u32[]{:S(2)}) %collective-permute-start.1) | collective-permute-done | bytes 786464 | tf_op jit(solution)/shard_map/ppermute | solution.py:63
  35.2 41.9 %all-gather.4.cloned.1.call-done = bf16[256,2,3072]{2,0,1:T(8,128)(2,1)} async-done(((bf16[64,2,3072]{2,0,1:T(8,128)(2,1)}), bf16[256,2,3072]{2,0,1:T(8,128)(2,1)}) %all-gather.4.cloned.1.call-update) | async-done | bytes 3145744 | tf_op jit(solution)/shard_map/all_gather | solution.py:21
  77.1 37.7 %all-gather.6.cloned.1.call-done = bf16[3072,1,768]{2,0,1:T(8,128)(2,1)} async-done(((bf16[768,1,768]{2,0,1:T(8,128)(2,1)}), bf16[3072,1,768]{2,0,1:T(8,128)(2,1)}) %all-gather.6.cloned.1.call-update) | async-done | bytes 4718608 | tf_op jit(solution)/shard_map/all_gather | solution.py:25
  114.7 5.9 %fusion = f32[256,2,768]{2,0,1:T(8,128)S(1)} fusion(bf16[256,2,3072]{2,0,1:T(8,128)(2,1)} %all-gather.4.cloned.1.call-done, bf16[3072,1,768]{2,0,1:T(8,128)(2,1)} %all-gather.6.cloned.1.call-done), kind=kOutput, calls=%fused_computation | convolution fusion | flops 2415919104 | bytes 9437184 | tf_op jit(solution)/shard_map/qye,ea->qya/dot_general | solution.py:22
  120.9 1.7 fusion.13
  122.6 0.4 multiply_reduce_fusion.1
  123.0 0.5 fusion.32
  123.8 0.4 broadcast_in_dim.2
  124.2 0.7 copy-done.3
  124.9 0.6 convolution_dynamic-update-slice_fusion.3
  125.5 0.6 copy-done.5
  126.1 0.6 convolution_dynamic-update-slice_fusion.2
  126.7 1.7 convolution_dynamic-update-slice_fusion.1
  128.4 1.7 convolution_dynamic-update-slice_fusion
  130.1 1.6 copy-done
  131.8 60.6 %reduce-scatter.2.cloned.1.call-done = bf16[64,2,3072]{2,0,1:T(8,128)(2,1)} async-done(((bf16[256,2,3072]{2,0,1:T(8,128)(2,1)}), bf16[64,2,3072]{2,0,1:T(8,128)(2,1)}) %reduce-scatter.2.cloned.1.call-update) | async-done | bytes 786448 | tf_op jit(solution)/shard_map/reduce_scatter | solution.py:75
  192.3 1.6 fusion.7
  193.9 1.7 copy.11
  (30 shorter events, 0.7 us)
Async XLA Ops:
  6.5 2.9 %copy-start.1 = (bf16[64,2,3072]{2,1,0:T(2,128)(2,1)S(1)}, bf16[64,2,3072]{2,1,0:T(2,128)(2,1)}, u32[]{:S(2)}) copy-start(bf16[64,2,3072]{2,1,0:T(2,128)(2,1)} %param.6) | copy-start | bytes 2359300
  6.5 2.9 %copy-start.6 = (f32[3072]{0:T(1024)S(1)}, f32[3072]{0:T(1024)}, u32[]{:S(2)}) copy-start(f32[3072]{0:T(1024)} %param.7) | copy-start | bytes 36868
  6.5 70.5 %all-gather.4.cloned.1.call-start = ((), (), s32[]{:S(2)}) async-start(), calls=%async_computation.1 | async-start | bytes 3932160 | tf_op jit(solution)/shard_map/all_gather | solution.py:21
  9.5 2.1 %copy-start.2 = (bf16[1,512,768]{2,1,0:T(8,128)(2,1)S(1)}, bf16[1,512,768]{2,1,0:T(8,128)(2,1)}, u32[]{:S(2)}) copy-start(bf16[1,512,768]{2,1,0:T(8,128)(2,1)} %param.11) | copy-start | bytes 2359300
  10.7 104.0 %all-gather.6.cloned.1.call-start = ((), (), s32[]{:S(2)}) async-start(), calls=%async_computation.3 | async-start | bytes 5898240 | tf_op jit(solution)/shard_map/all_gather | solution.py:25
  11.5 180.9 %reduce-scatter.2.cloned.1.call-start = ((), (), s32[]{:S(2)}) async-start(), calls=%async_computation.2 | async-start | bytes 3932160 | tf_op jit(solution)/shard_map/reduce_scatter | solution.py:75
  11.5 12.1 %collective-permute-start = (bf16[512,768]{1,0:T(8,128)(2,1)S(1)}, bf16[512,768]{1,0:T(8,128)(2,1)S(1)}, u32[]{:S(2)}, u32[]{:S(2)}) collective-permute-start(bf16[512,768]{1,0:T(8,128)(2,1)S(1)} %bitcast.28), channel_id=1, source_target_pairs={{0,1},{1,2},{2,3},{3,0},{4,5},{5,6},{6,7},{7,4},{8,9},{9,10},{10,1... | collective-permute-start | bytes 2359304 | tf_op jit(solution)/shard_map/ppermute | solution.py:63
  23.7 96.9 %copy-start.4 = (bf16[512,768]{1,0:T(8,128)(2,1)}, bf16[512,768]{1,0:T(8,128)(2,1)S(1)}, u32[]{:S(2)}) copy-start(bf16[512,768]{1,0:T(8,128)(2,1)S(1)} %collective-permute-done) | copy-start | bytes 2359300
  23.7 11.5 %collective-permute-start.1 = (bf16[512,768]{1,0:T(8,128)(2,1)S(1)}, bf16[512,768]{1,0:T(8,128)(2,1)}, u32[]{:S(2)}, u32[]{:S(2)}) collective-permute-start(bf16[512,768]{1,0:T(8,128)(2,1)S(1)} %collective-permute-done), channel_id=1, source_target_pairs={{0,1},{1,2},{2,3},{3,0},{4,5},{5,6},{6,7},{7,4},{8,9},{9,10},{10,1... | collective-permute-start | bytes 2359304 | tf_op jit(solution)/shard_map/ppermute | solution.py:63
  35.2 93.2 %collective-permute-start.2 = (bf16[512,768]{1,0:T(8,128)(2,1)}, bf16[512,768]{1,0:T(8,128)(2,1)}, u32[]{:S(2)}, u32[]{:S(2)}) collective-permute-start(bf16[512,768]{1,0:T(8,128)(2,1)} %collective-permute-done.1), channel_id=1, source_target_pairs={{0,1},{1,2},{2,3},{3,0},{4,5},{5,6},{6,7},{7,4},{8,9},{9,10},{10,1... | collective-permute-start | bytes 2359304 | tf_op jit(solution)/shard_map/ppermute | solution.py:63
  120.6 2.4 %copy-start.7 = (f32[1,128]{1,0:T(1,128)S(1)}, f32[1,128]{1,0:T(1,128)}, u32[]{:S(2)}) copy-start(f32[1,128]{1,0:T(1,128)} %param.10) | copy-start | bytes 1540
  120.6 2.4 %copy-start.8 = (f32[1,128]{1,0:T(1,128)S(1)}, f32[1,128]{1,0:T(1,128)}, u32[]{:S(2)}) copy-start(f32[1,128]{1,0:T(1,128)} %param.9) | copy-start | bytes 1540
  123.8 1.1 copy-start.3
  124.9 1.1 copy-start.5
  130.1 1.7 copy-start
Sparse Core Ops, SparseCore 0:
  10.9 66.1 all-gather.3
  78.6 36.0 all-gather.5
  131.9 60.3 reduce-scatter.1
